TPU v7x, 128 devices: a whole 4x4x4 slice. The times are simulated.
128 devices in a mesh: row: 16 (over y_hi, z, core), col: 8 (over y_lo, x).
Axes of the slice: x: 4, y: 4 (y_hi: 2, y_lo: 2; y = y_hi * 2 + y_lo), z: 4, core: 2. Of those that a mesh axis runs over, the one named last changes fastest.
Arguments:
- gate_input: bfloat16 [2, 1024, 53248], P(None, 'col', 'row'), may hold values from -6 to 6
- up_input: bfloat16 [2, 1024, 53248], P(None, 'col', 'row'), may hold values from -6 to 6
- down_weight: bfloat16 [53248, 16384], P('row', 'col'), may hold values from -0.02734375 to 0.02734375
Outputs:
- mixed: bfloat16 [2, 1024, 16384], P(None, 'row', 'col')
All inputs are finite; a program needn't handle non-finite values.
Results may differ from a plain program's by a relative error of at most 0.0049.
Values may be sent and summed in bfloat16 or wider, within the bound.
A program may use at most 128 MiB of HBM per device.

v0:
```python
import jax
import jax.numpy as jnp
from jax import lax
from jax.sharding import PartitionSpec as P


def gated_hidden(gate_part, up_part):
    product = jax.nn.silu(gate_part.astype(jnp.float32)) * up_part.astype(jnp.float32)
    return product.astype(jnp.bfloat16)


def gathered_hidden(gate_part, up_part):
    return lax.all_gather(gated_hidden(gate_part, up_part), "col", axis=1, tiled=True)


def body(gate_input, up_input, down_weight):
    hidden_units = down_weight.shape[0]
    width = down_weight.shape[1]
    hidden = gathered_hidden(gate_input, up_input)
    seq_count = hidden.shape[0]
    seq_tokens = hidden.shape[1]
    flat = hidden.reshape(seq_count * seq_tokens, hidden_units)
    partial_value = jnp.dot(flat, down_weight, preferred_element_type=jnp.float32)
    partial_value = partial_value.reshape(seq_count, seq_tokens, width)
    mixed = lax.psum_scatter(partial_value, "row", scatter_dimension=1, tiled=True)
    return mixed.astype(jnp.bfloat16)


def solution(mesh):
    return jax.shard_map(
        body,
        mesh=mesh,
        in_specs=(P(None, "col", "row"), P(None, "col", "row"), P("row", "col")),
        out_specs=P(None, "row", "col"),
        check_vma=False,
    )
```

profile of v0, /device:TPU:0, one launch (start us, length us, event | category | flops | bytes accessed | tf_op | source)
XLA Modules:
  0.0 345.1 jit_solution(2053406622738443245)
XLA Ops:
  6.5 0.0 all-gather.2.cloned.1.call-start
  6.5 4.2 %fusion.6 = bf16[2,128,3328]{2,1,0:T(8,128)(2,1)} fusion(bf16[2,128,3328]{2,1,0:T(8,128)(2,1)} %param.4, bf16[2,128,3328]{2,1,0:T(8,128)(2,1)} %param.3), kind=kLoop, calls=%fused_computation.8 | loop fusion | flops 6815744 | bytes 5111808 | tf_op jit(solution)/shard_map/convert_element_type | solution.py:9
  10.7 0.0 all-gather.2.cloned.1.call-update
  10.7 0.0 reduce-scatter.2.cloned.1.call-start
  10.8 143.6 %all-gather.2.cloned.1.call-done = bf16[2,1024,3328]{2,1,0:T(8,128)(2,1)} async-done(((bf16[2,128,3328]{2,1,0:T(8,128)(2,1)}), bf16[2,1024,3328]{2,1,0:T(8,128)(2,1)}) %all-gather.2.cloned.1.call-update) | async-done | bytes 13631504 | tf_op jit(solution)/shard_map/all_gather | solution.py:13
  154.4 35.6 %fusion = f32[2,1024,2048]{2,1,0:T(8,128)} fusion(bf16[2,1024,3328]{2,1,0:T(8,128)(2,1)} %all-gather.2.cloned.1.call-done, bf16[3328,2048]{1,0:T(8,128)(2,1)} %param.5), kind=kOutput, calls=%fused_computation | convolution fusion | flops 27917287424 | bytes 44040192 | tf_op jit(solution)/shard_map/dot_general | solution.py:23
  190.0 0.0 reduce-scatter.2.cloned.1.call-update
  190.0 146.2 %reduce-scatter.2.cloned.1.call-done = f32[2,64,2048]{2,1,0:T(8,128)} async-done(((f32[2,1024,2048]{2,1,0:T(8,128)}), f32[2,64,2048]{2,1,0:T(8,128)}) %reduce-scatter.2.cloned.1.call-update) | async-done | bytes 1048592 | tf_op jit(solution)/shard_map/reduce_scatter | solution.py:25
  336.2 2.1 convert_element_type.15
Async XLA Ops:
  6.5 147.8 %all-gather.2.cloned.1.call-start = ((), (), s32[]{:S(2)}) async-start(), calls=%async_computation.1 | async-start | bytes 15335424 | tf_op jit(solution)/shard_map/all_gather | solution.py:13
  10.7 325.5 %reduce-scatter.2.cloned.1.call-start = ((), (), s32[]{:S(2)}) async-start(), calls=%async_computation.2 | async-start | bytes 17825792 | tf_op jit(solution)/shard_map/reduce_scatter | solution.py:25
Sparse Core Ops, SparseCore 0:
  10.9 143.4 all-gather.1
  190.1 146.0 reduce-scatter.1
where the time goes:
time: 345 us
  waiting for transfers between devices  290 us (84%)
  matrix products  35.6 us (10%)
  between operations  13.4 us (4%)
  other arithmetic  6.26 us (2%)
    reduce_scatter x1, waiting for transfers between devices, body(): lax.psum_scatter(partial_value, 'row', scatter_dimension=1, tiled=True)  146 us
    all_gather x1, waiting for transfers between devices, gathered_hidden(): lax.all_gather(gated_hidden(gate_part, up_part), 'col', axis=1, tiled=True)  144 us
    dot_general x1, matrix products, body(): jnp.dot(flat, down_weight, preferred_element_type=jnp.float32)  35.6 us
  transfers between devices with their start and end apart: 2, of which 2 were waited for; matrix products, arithmetic and copies ran while one was open for 0% of the time, Pallas kernels for 0%

commit v1 on v0

--- a/solution.py
+++ b/solution.py
@@ -2,6 +2,11 @@
 import jax.numpy as jnp
 from jax import lax
 from jax.sharding import PartitionSpec as P
+
+
+def exchange_gather(array, name, dim):
+    sent = jnp.stack([array] * lax.axis_size(name))
+    return jnp.concatenate(lax.all_to_all(sent, name, 0, 0), axis=dim)
 
 
 def gated_hidden(gate_part, up_part):
@@ -10,7 +15,7 @@
 
 
 def gathered_hidden(gate_part, up_part):
-    return lax.all_gather(gated_hidden(gate_part, up_part), "col", axis=1, tiled=True)
+    return exchange_gather(gated_hidden(gate_part, up_part), "col", 1)
 
 
 def body(gate_input, up_input, down_weight):

time: 345 us -> 366 us (1.061)
  blocking collectives: 0 us -> 158 us
  waiting for transfers between devices: 290 us -> 148 us
  local copies, waits for them, and re-layouts: 0 us -> 8.27 us
    all_to_all x0 -> x1, blocking collectives: none -> 158 us  [exchange_gather(): return jnp.concatenate(lax.all_to_all(sent, name, 0, 0), axis=dim)]
    all_gather x1 -> x0, waiting for transfers between devices: 144 us -> none  [gathered_hidden(): lax.all_gather(gated_hidden(gate_part, up_part), 'col', axis=1, tiled=True)]
    another operation x0 -> x1, local copies, waits for them, and re-layouts: none -> 6.2 us  [exchange_gather(): sent = jnp.stack([array] * lax.axis_size(name))]
  transfers between devices with their start and end apart: 2 -> 1, of which waited for: 2 -> 1; matrix products, arithmetic and copies ran while one was open for 0% -> 0% of each run, Pallas kernels for 0% -> 0%
where the time goes in v1:
time: 366 us
  blocking collectives  158 us (43%)
  waiting for transfers between devices  148 us (40%)
  matrix products  33.6 us (9%)
  between operations  13.4 us (4%)
  local copies, waits for them, and re-layouts  8.27 us (2%)
  other arithmetic  5.06 us (1%)
    all_to_all x1, blocking collectives, exchange_gather(): return jnp.concatenate(lax.all_to_all(sent, name, 0, 0), axis=dim)  158 us
    reduce_scatter x1, waiting for transfers between devices, body(): lax.psum_scatter(partial_value, 'row', scatter_dimension=1, tiled=True)  148 us
    dot_general x1, matrix products, body(): jnp.dot(flat, down_weight, preferred_element_type=jnp.float32)  33.6 us
  transfers between devices with their start and end apart: 1, of which 1 were waited for; matrix products, arithmetic and copies ran while one was open for 0% of the time, Pallas kernels for 0%

profile of v1, /device:TPU:0, one launch (start us, length us, event | category | flops | bytes accessed | tf_op | source)
XLA Modules:
  0.0 366.0 jit_solution(1355126779133044847)
XLA Ops:
  6.5 0.0 reduce-scatter.2.cloned.1.call-start
  6.5 3.0 fusion.6
  9.5 6.2 %stack.2 = bf16[8,2,128,3328]{3,2,1,0:T(8,128)(2,1)} broadcast(bf16[2,128,3328]{2,1,0:T(8,128)(2,1)S(1)} %fusion.6), dimensions={1,2,3} | broadcast | bytes 15335424 | tf_op jit(solution)/shard_map/stack | solution.py:8
  15.7 157.7 %all_to_all.5 = bf16[8,2,128,3328]{3,2,1,0:T(8,128)(2,1)S(1)} all-to-all(bf16[8,2,128,3328]{3,2,1,0:T(8,128)(2,1)} %stack.2), channel_id=1, replica_groups=mesh['row'=16,'col'=8] {'col'}, dimensions={0} | all-to-all | bytes 27262976 | tf_op jit(solution)/shard_map/all_to_all | solution.py:9
  173.4 2.1 copy.4
  175.5 33.6 %fusion = f32[2,1024,2048]{2,1,0:T(8,128)} fusion(bf16[2,1024,3328]{2,1,0:T(8,128)(2,1)S(1)} %bitcast.7, bf16[3328,2048]{1,0:T(8,128)(2,1)} %param.5), kind=kOutput, calls=%fused_computation | convolution fusion | flops 27917287424 | bytes 44040192 | tf_op jit(solution)/shard_map/dot_general | solution.py:28
  209.0 0.0 reduce-scatter.2.cloned.1.call-update
  209.1 148.0 %reduce-scatter.2.cloned.1.call-done = f32[2,64,2048]{2,1,0:T(8,128)} async-done(((f32[2,1024,2048]{2,1,0:T(8,128)}), f32[2,64,2048]{2,1,0:T(8,128)}) %reduce-scatter.2.cloned.1.call-update) | async-done | bytes 1048592 | tf_op jit(solution)/shard_map/reduce_scatter | solution.py:30
  357.1 2.1 convert_element_type.15
Async XLA Ops:
  6.5 350.6 %reduce-scatter.2.cloned.1.call-start = ((), (), s32[]{:S(2)}) async-start(), calls=%async_computation.2 | async-start | bytes 17825792 | tf_op jit(solution)/shard_map/reduce_scatter | solution.py:30
Sparse Core Ops, SparseCore 0:
  209.2 147.8 reduce-scatter.1
